TPU v7x, 32 devices: a whole 2x2x4 slice. The times are simulated.
32 devices in a mesh: row: 4 (over y, core), col: 8 (over z, x).
Axes of the slice: x: 2, y: 2, z: 4, core: 2. Of those that a mesh axis runs over, the one named last changes fastest.
Arguments:
- coupling_panel: bfloat16 [4, 1536, 512], P('row'), may hold values from -6 to 6
- interior_factor: float32 [4, 1536, 1536], P('row'), may hold values from -1 to 3, as said below
- border_rows: bfloat16 [4, 4096, 1536], P('row', 'col'), may hold values from -0.109375 to 0.109375
- target_rows: int32 [4, 4096], P('row', 'col'), may hold values from 0 to 8191, as said below
- border_block: float32 [8192, 512], P(('row', 'col')), may hold values from -6 to 6
Outputs:
- schur_panel: float32 [8192, 512], P(('row', 'col'))
Inputs may be any that keep to these rules, and one draw needn't show every extreme that they name: `target_rows`: each block of 512 entries along the second dimension (the rows of one device) is nondecreasing. Row g of the Schur panel is held by device g // 256 in the order of row+col. The rows of one device name any one holder at most 32 times, and some holder is named exactly 32 times by the rows of every device. `interior_factor`: each [1536, 1536] block is lower triangular with diagonal entries between 1 and 3.
All inputs are finite; a program needn't handle non-finite values.
Results may differ from a plain program's by a relative error of at most 0.0029.
Values may be sent and summed in bfloat16 or wider, within the bound.
A program may use at most 128 MiB of HBM per device.

v0:
```python
import jax
import jax.numpy as jnp
from jax import lax
from jax.sharding import PartitionSpec as P


def substitute(factor, panel_cols):
    forward = lax.linalg.triangular_solve(factor, panel_cols, left_side=True, lower=True)
    return lax.linalg.triangular_solve(
        factor, forward, left_side=True, lower=True, transpose_a=True
    )


def local(coupling_panel, interior_factor, border_rows, target_rows, border_block):
    factor = interior_factor[0]
    panel_cols = coupling_panel[0]
    coupling_rows = border_rows[0]
    targets = target_rows[0]
    panel_width = panel_cols.shape[1]
    holders = lax.axis_size("row") * lax.axis_size("col")
    owned_rows = border_block.shape[0]
    sent_rows = targets.shape[0]
    slot_depth = 2 * sent_rows // holders
    holder_of = targets // owned_rows
    onehot = (holder_of[:, None] == jnp.arange(holders, dtype=jnp.int32)[None, :]).astype(jnp.int32)
    counts = jnp.sum(onehot, axis=0)
    starts = jnp.cumsum(counts) - counts
    start_of = jnp.sum(onehot * starts[None, :], axis=1)
    slot_rank = jnp.arange(sent_rows, dtype=jnp.int32) - start_of
    position = holder_of * slot_depth + slot_rank
    within = targets - holder_of * owned_rows
    send_index = jnp.zeros((holders * slot_depth,), jnp.int32).at[position].set(within)
    recv_index = lax.all_to_all(
        send_index.reshape(holders, slot_depth),
        ("row", "col"),
        split_axis=0,
        concat_axis=0,
        tiled=True,
    )
    solved = substitute(factor, panel_cols.astype(jnp.float32)).astype(jnp.bfloat16)
    update = jnp.dot(coupling_rows, solved, preferred_element_type=jnp.float32)
    outgoing = jnp.zeros((holders * slot_depth, panel_width), jnp.float32).at[position].set(update)
    received = lax.all_to_all(
        outgoing.reshape(holders, slot_depth, panel_width),
        ("row", "col"),
        split_axis=0,
        concat_axis=0,
        tiled=True,
    )
    received = received.reshape(holders * slot_depth, panel_width)
    assembled = (
        jnp.zeros((owned_rows, panel_width), jnp.float32).at[recv_index.reshape(-1)].add(received)
    )
    return border_block - assembled


def solution(mesh):
    placed = (
        P("row", None, None),
        P("row", None, None),
        P("row", "col", None),
        P("row", "col"),
        P(("row", "col"), None),
    )
    return jax.shard_map(
        local, mesh=mesh, in_specs=placed, out_specs=P(("row", "col"), None), check_vma=False
    )
```

profile of v0, /device:TPU:0, one launch (start us, length us, event | category | flops | bytes accessed | tf_op | source)
XLA Modules:
  0.0 293.8 jit_solution(5810232975698918122)
XLA Ops:
  0.0 0.8 multiply_subtract_fusion
  1.3 0.7 compare_select_fusion.1
  2.0 2.4 scatter_custom_fusion
  4.5 0.7 all_to_all.9
  5.1 7.3 %all-to-all-start = ((s32[32,1,32]{2,1,0:T(1,128)}), s32[32,1,32]{2,1,0:T(1,128)S(1)}, u32[]{:S(2)}, u32[]{:S(2)}) async-start(s32[32,1,32]{2,1,0:T(1,128)} %all_to_all.9), calls=%async_computation | async-start | bytes 32768 | tf_op jit(solution)/shard_map/all_to_all | solution.py:33
  12.5 8.4 %bitcast_select_fusion = f32[1536,1536]{1,0:T(8,128)} fusion(f32[1,1536,1536]{2,1,0:T(8,128)} %param.6), kind=kLoop, calls=%fused_computation.5 | loop fusion | flops 4718592 | bytes 18874368 | tf_op jit(solution)/shard_map/triangular_solve | solution.py:9
  20.9 41.3 %while.1 = (s32[]{:T(128)}, f32[1536,1536]{1,0:T(8,128)}, s32[12,2]{0,1:T(2,128)S(1)}, f32[12,128,128]{2,1,0:T(8,128)}, s32[]{:T(128)}) while((s32[]{:T(128)}, f32[1536,1536]{1,0:T(8,128)}, s32[12,2]{0,1:T(2,128)S(1)}, f32[12,128,128]{2,1,0:T(8,128)}, s32[]{:T(128)}) %tuple.84), condition=%wide.while_cond, body=%wide.while_body.sunk | while | flops 2 | bytes 132705 | solution.py:9
  20.9 0.5 fusion.139
  21.5 2.8 bitcast_dynamic-update-slice_fusion.2
  24.4 0.5 fusion.139
  24.9 2.8 bitcast_dynamic-update-slice_fusion.2
  27.8 0.5 fusion.139
  28.4 2.8 bitcast_dynamic-update-slice_fusion.2
  31.3 0.5 fusion.139
  31.8 2.8 bitcast_dynamic-update-slice_fusion.2
  34.7 0.5 fusion.139
  35.3 2.8 bitcast_dynamic-update-slice_fusion.2
  38.2 0.5 fusion.139
  38.7 2.8 bitcast_dynamic-update-slice_fusion.2
  41.6 0.5 fusion.139
  42.2 2.8 bitcast_dynamic-update-slice_fusion.2
  45.1 0.5 fusion.139
  45.6 2.8 bitcast_dynamic-update-slice_fusion.2
  48.5 0.5 fusion.139
  49.1 2.8 bitcast_dynamic-update-slice_fusion.2
  52.0 0.5 fusion.139
  52.5 2.8 bitcast_dynamic-update-slice_fusion.2
  55.4 0.5 fusion.139
  56.0 2.8 bitcast_dynamic-update-slice_fusion.2
  58.9 0.5 fusion.139
  59.4 2.8 bitcast_dynamic-update-slice_fusion.2
  62.2 118.8 %custom-call.5 = f32[12,128,128]{1,2,0:T(8,128)S(1)} custom-call(f32[12,128,128]{2,1,0:T(8,128)} %get-tuple-element.12), custom_call_target="InvertDiagBlocksLowerTriangular" | custom-call | tf_op jit(solution)/shard_map/triangular_solve | solution.py:9
  181.1 2.0 convert_element_type.9
  183.0 1.7 constant_dynamic-update-slice_fusion.44
  184.8 1.2 convolution_subtract_fusion.11
  186.0 0.5 constant_dynamic-update-slice_fusion.43
  187.0 0.5 constant_dynamic-update-slice_fusion.42
  187.5 0.6 convolution_subtract_fusion.17
  188.7 0.7 convolution_subtract_fusion.21
  189.4 0.5 constant_dynamic-update-slice_fusion.40
  190.0 0.9 convolution_subtract_fusion.9
  191.4 1.0 convolution_subtract_fusion.16
  192.9 1.2 convolution_subtract_fusion.8
  194.6 1.3 convolution_subtract_fusion.7
  196.4 1.5 convolution_subtract_fusion.15
  198.3 1.8 convolution_subtract_fusion.20
  200.6 1.8 convolution_subtract_fusion.6
  204.8 0.7 convolution_subtract_fusion.14
  205.9 0.8 convolution_subtract_fusion.19
  207.2 1.0 convolution_subtract_fusion.3
  208.7 1.1 convolution_subtract_fusion.13
  210.4 1.3 convolution_subtract_fusion.2
  212.3 1.9 convolution_subtract_fusion.1
  214.7 1.6 convolution_subtract_fusion.12
  217.0 1.8 convolution_subtract_fusion.18
  219.4 2.0 convolution_subtract_fusion
  222.0 2.0 fusion.2
  224.1 1.6 copy.11
  225.6 3.6 %scatter_custom_fusion.1 = f32[1024,512]{1,0:T(8,128)} fusion(s32[512]{0:T(512)S(1)} %bitcast.214, f32[512,512]{1,0:T(8,128)S(1)} %copy.11, f32[]{:T(128)} %constant.36.clone.1), kind=kCustom, calls=%fused_computation.48 | custom fusion | bytes 2097156 | tf_op jit(solution)/shard_map/scatter | solution.py:42
  229.3 6.1 %all-to-all-start.1 = ((f32[32,32,512]{2,1,0:T(8,128)}), f32[32,32,512]{2,1,0:T(8,128)}, u32[]{:S(2)}, u32[]{:S(2)}) async-start(f32[32,32,512]{2,1,0:T(8,128)} %bitcast.209), calls=%async_computation.1 | async-start | bytes 4194304 | tf_op jit(solution)/shard_map/all_to_all | solution.py:43
  235.9 0.7 reduce.4
  236.7 48.6 %all-to-all-done.1 = f32[32,32,512]{2,1,0:T(8,128)} async-done(((f32[32,32,512]{2,1,0:T(8,128)}), f32[32,32,512]{2,1,0:T(8,128)}, u32[]{:S(2)}, u32[]{:S(2)}) %all-to-all-start.1) | async-done | bytes 2097184 | tf_op jit(solution)/shard_map/all_to_all | solution.py:43
  285.3 7.5 %scatter_custom_fusion.2 = f32[256,512]{1,0:T(8,128)S(1)} fusion(s32[1024]{0:T(1024)S(1)} %bitcast.212, f32[1024,512]{1,0:T(8,128)} %bitcast.34, f32[]{:T(128)} %constant.36.clone.1), kind=kCustom, calls=%fused_computation.93 | custom fusion | flops 524288 | bytes 524800 | tf_op jit(solution)/shard_map/scatter-add | solution.py:52
  292.8 0.9 sub.36
  (114 shorter events, 12.6 us)
Async XLA Ops:
  0.0 222.0 %copy-start = (bf16[1,512,1536]{2,1,0:T(8,128)(2,1)S(1)}, bf16[1,512,1536]{2,1,0:T(8,128)(2,1)}, u32[]{:S(2)}) copy-start(bf16[1,512,1536]{2,1,0:T(8,128)(2,1)} %param.7) | copy-start | bytes 4718596
  5.1 224.1 %all-to-all-start = ((s32[32,1,32]{2,1,0:T(1,128)}), s32[32,1,32]{2,1,0:T(1,128)S(1)}, u32[]{:S(2)}, u32[]{:S(2)}) async-start(s32[32,1,32]{2,1,0:T(1,128)} %all_to_all.9), calls=%async_computation | async-start | bytes 32768 | tf_op jit(solution)/shard_map/all_to_all | solution.py:33
  181.0 5.5 %copy-start.1 = (f32[1536,1536]{1,0:T(8,128)S(1)}, f32[1536,1536]{1,0:T(8,128)}, u32[]{:S(2)}) copy-start(f32[1536,1536]{1,0:T(8,128)} %get-tuple-element.152) | copy-start | bytes 28311556
  229.3 63.5 %copy-start.2 = (f32[256,512]{1,0:T(8,128)S(1)}, f32[256,512]{1,0:T(8,128)}, u32[]{:S(2)}) copy-start(f32[256,512]{1,0:T(8,128)} %param.9) | copy-start | bytes 1572868
  229.3 56.0 %all-to-all-start.1 = ((f32[32,32,512]{2,1,0:T(8,128)}), f32[32,32,512]{2,1,0:T(8,128)}, u32[]{:S(2)}, u32[]{:S(2)}) async-start(f32[32,32,512]{2,1,0:T(8,128)} %bitcast.209), calls=%async_computation.1 | async-start | bytes 4194304 | tf_op jit(solution)/shard_map/all_to_all | solution.py:43
where the time goes:
time: 299 us; the launch traced here: 294 us
  other arithmetic  140 us (47%)
  local copies, waits for them, and re-layouts  51.3 us (17%)
  waiting for transfers between devices  48.6 us (16%)
  matrix products  39 us (13%)
  starting transfers between devices  13.5 us (5%)
    another operation x4, other arithmetic, substitute(): lax.linalg.triangular_solve(factor, forward, left_side=True, lower=True,...  127 us
    all_to_all x1, waiting for transfers between devices, local(): lax.all_to_all(outgoing.reshape(holders, slot_depth, panel_width), ('row'...  48.6 us
    another operation x37, local copies, waits for them, and re-layouts  41.4 us
    another operation x23, matrix products, substitute(): lax.linalg.triangular_solve(factor, panel_cols, left_side=True, lower=True)  19.5 us
    another operation x23, matrix products, substitute(): lax.linalg.triangular_solve(factor, forward, left_side=True, lower=True,...  17.4 us
    scatter-add x1, other arithmetic, local(): jnp.zeros((owned_rows, panel_width), jnp.float32).at[recv_index.reshape(-1)]  7.46 us
    all_to_all x1, starting transfers between devices, local(): lax.all_to_all(send_index.reshape(holders, slot_depth), ('row', 'col'), s...  7.33 us
    all_to_all x1, starting transfers between devices, local(): lax.all_to_all(outgoing.reshape(holders, slot_depth, panel_width), ('row'...  6.13 us
  transfers between devices with their start and end apart: 2, of which 1 were waited for; matrix products, arithmetic and copies ran while one was open for 74% of the time, Pallas kernels for 0%

commit v1 on v0

v1 whole, which is shorter than its diff:
```python
import functools

import jax
import jax.numpy as jnp
from jax import lax
from jax.experimental import pallas as pl
from jax.experimental.pallas import tpu as pltpu
from jax.sharding import PartitionSpec as P

F32 = jnp.float32
BF16 = jnp.bfloat16
BASE = 16
LANES = 128
BLOCK = 256
NN = (((1,), (0,)), ((), ()))
TN = (((0,), (0,)), ((), ()))


def iota(shape, dim):
    return lax.broadcasted_iota(jnp.int32, shape, dim)


def split(x):
    high = x.astype(BF16)
    return high, (x - high.astype(F32)).astype(BF16)


def dot(a, b, dims=NN):
    return lax.dot_general(a, b, dims, preferred_element_type=F32)


def dot3(a, b, dims=NN):
    return dot(a[0], b[0], dims) + (dot(a[0], b[1], dims) + dot(a[1], b[0], dims))


def invert_bases(factor_ref, small_ref):
    chunks = factor_ref.shape[0] // LANES
    padded = small_ref.shape[1]
    small_ref[...] = jnp.ones(small_ref.shape, F32)
    same = iota((LANES, LANES), 0) // BASE == iota((LANES, LANES), 1) // BASE
    for k in range(chunks):
        here = pl.ds(k * LANES, LANES)
        diag = jnp.where(same, factor_ref[here, here], 0.0)
        small_ref[:, k, :] = jnp.sum(diag.reshape(LANES // BASE, BASE, LANES), axis=0)
    rows = small_ref[...].reshape(BASE * padded, LANES)
    high = rows.astype(BF16)
    rest = rows - high.astype(F32)
    mid = rest.astype(BF16)
    low = (rest - mid.astype(F32)).astype(BF16)
    pair = jnp.concatenate([high, mid], axis=1)
    lane = iota((padded, LANES), 1) % BASE
    source = iota((2 * LANES, LANES), 0) % LANES
    target = iota((2 * LANES, LANES), 1)
    solved = []
    coefs = []
    for j in range(BASE):
        spread = ((source // BASE == target // BASE) & (source % BASE == j)).astype(BF16)
        first = j * padded
        coefs.append(dot(pair[first:], spread) + dot(low[first:], spread[:LANES]))
    for i in range(BASE):
        acc = (lane == i).astype(F32)
        for j in range(i):
            at = (i - j) * padded
            acc -= coefs[j][at : at + padded] * solved[j]
        solved.append(acc / coefs[i][:padded])
    for i in range(BASE):
        small_ref[i] = solved[i]


def invert_blocks(factor_ref, small_ref, inv_hi, inv_lo):
    blocks = factor_ref.shape[0] // BLOCK
    row, col = iota((BLOCK, BLOCK), 0), iota((BLOCK, BLOCK), 1)
    per = BLOCK // LANES
    inverses = []
    for p in range(blocks):
        parts = []
        for h in range(per):
            compact = small_ref[:, p * per + h, :]
            parts.append(jnp.concatenate([compact] * (LANES // BASE), axis=0))
        tall = jnp.concatenate(parts, axis=0)
        wide = jnp.concatenate([tall] * per, axis=1)
        inverses.append(jnp.where(row // BASE == col // BASE, wide, 0.0))
    size = BASE
    while size < BLOCK:
        off = (row // (2 * size) == col // (2 * size)) & (row // size != col // size) & (row > col)
        for p in range(blocks):
            here = pl.ds(p * BLOCK, BLOCK)
            below = split(jnp.where(off, factor_ref[here, here], 0.0))
            inverse = split(inverses[p])
            inverses[p] = inverses[p] - dot3(inverse, split(dot3(below, inverse)))
        size *= 2
    for p in range(blocks):
        inv_hi[p], inv_lo[p] = split(inverses[p])


def split_factor(factor_ref, l_hi, l_lo):
    blocks = factor_ref.shape[0] // BLOCK
    for k in range(1, blocks):
        at = (pl.ds(k * BLOCK, BLOCK), pl.ds(0, k * BLOCK))
        l_hi[at], l_lo[at] = split(factor_ref[at])


def substitute(panel, l_hi, l_lo, inv_hi, inv_lo, x_hi, x_lo):
    blocks = inv_hi.shape[0]
    for k in range(blocks):
        here, done = pl.ds(k * BLOCK, BLOCK), pl.ds(0, k * BLOCK)
        acc = panel(here).astype(F32)
        if k:
            acc -= dot3((l_hi[here, done], l_lo[here, done]), (x_hi[done, :], x_lo[done, :]))
        x_hi[here, :], x_lo[here, :] = split(dot3((inv_hi[k], inv_lo[k]), split(acc)))
    for k in reversed(range(blocks)):
        here = pl.ds(k * BLOCK, BLOCK)
        done = pl.ds((k + 1) * BLOCK, (blocks - 1 - k) * BLOCK)
        acc = x_hi[here, :].astype(F32) + x_lo[here, :].astype(F32)
        if k < blocks - 1:
            acc -= dot3((l_hi[done, here], l_lo[done, here]), (x_hi[done, :], x_lo[done, :]), TN)
        x_hi[here, :], x_lo[here, :] = split(dot3((inv_hi[k], inv_lo[k]), split(acc), TN))


def slots_of(targets, holders, depth, owned):
    rows = targets.shape[1]
    holder = targets // owned
    ids = iota((holders, rows), 0)
    counts = jnp.sum((ids == holder).astype(F32), axis=1, keepdims=True)
    start = jnp.sum(jnp.where(ids < holder, counts, 0.0), axis=0, keepdims=True).astype(jnp.int32)
    position = holder * depth + iota((1, rows), 1) - start
    return iota((holders * depth, rows), 0) == position


def solve_kernel(holders, depth, owned, factor_ref, panel_ref, border_ref, targets_ref, out_ref,
                 small_ref, inv_hi, inv_lo, l_hi, l_lo, x_hi, x_lo, slots_ref):
    slots = slots_of(targets_ref[...], holders, depth, owned)
    slots_ref[...] = jnp.where(slots, 1.0, 0.0).astype(BF16)
    invert_bases(factor_ref, small_ref)
    invert_blocks(factor_ref, small_ref, inv_hi, inv_lo)
    split_factor(factor_ref, l_hi, l_lo)
    substitute(lambda at: panel_ref[at, :], l_hi, l_lo, inv_hi, inv_lo, x_hi, x_lo)
    update = dot(border_ref[...], x_hi[...]).astype(BF16)
    out_ref[...] = dot(slots_ref[...], update).astype(BF16)


def solve(holders, depth, owned, factor, panel, border, targets):
    n, width = panel.shape
    vmem = pl.BlockSpec(memory_space=pltpu.VMEM)
    padded = -(-(n // LANES) // 8) * 8
    return pl.pallas_call(
        functools.partial(solve_kernel, holders, depth, owned),
        out_shape=jax.ShapeDtypeStruct((holders * depth, width), BF16),
        in_specs=[vmem] * 4,
        out_specs=vmem,
        scratch_shapes=[
            pltpu.VMEM((BASE, padded, LANES), F32),
            pltpu.VMEM((n // BLOCK, BLOCK, BLOCK), BF16),
            pltpu.VMEM((n // BLOCK, BLOCK, BLOCK), BF16),
            pltpu.VMEM((n, n), BF16),
            pltpu.VMEM((n, n), BF16),
            pltpu.VMEM((n, width), BF16),
            pltpu.VMEM((n, width), BF16),
            pltpu.VMEM((holders * depth, border.shape[0]), BF16),
        ],
        compiler_params=pltpu.CompilerParams(vmem_limit_bytes=60 * 2**20),
        cost_estimate=pl.CostEstimate(flops=10**10, bytes_accessed=14 * 10**6, transcendentals=0),
        name="solve",
    )(factor, panel, border, targets)


def gather_kernel(owned, index_ref, received_ref, block_ref, out_ref):
    slots = received_ref.shape[0]
    pick = iota((owned, slots), 0) == index_ref[...]
    pick = jnp.where(pick, 1.0, 0.0).astype(BF16)
    out_ref[...] = block_ref[...] - dot(pick, received_ref[...])


def gather(index, received, block):
    vmem = pl.BlockSpec(memory_space=pltpu.VMEM)
    return pl.pallas_call(
        functools.partial(gather_kernel, block.shape[0]),
        out_shape=jax.ShapeDtypeStruct(block.shape, F32),
        in_specs=[vmem] * 3,
        out_specs=vmem,
        compiler_params=pltpu.CompilerParams(vmem_limit_bytes=40 * 2**20),
        name="gather",
    )(index, received, block)


def local(coupling_panel, interior_factor, border_rows, target_rows, border_block):
    holders = lax.axis_size("row") * lax.axis_size("col")
    owned = border_block.shape[0]
    targets = target_rows[0]
    sent = targets.shape[0]
    depth = 2 * sent // holders
    width = border_block.shape[1]
    holder_of = targets // owned
    ids = jnp.arange(holders, dtype=jnp.int32)
    start = jnp.sum((holder_of[None, :] < ids[:, None]).astype(jnp.int32), axis=1)
    first = start[:, None] + jnp.arange(depth, dtype=jnp.int32)[None, :]
    wanted = targets[jnp.minimum(first, sent - 1)]
    valid = (first < sent) & (wanted // owned == ids[:, None])
    send_index = jnp.where(valid, wanted % owned, -1)
    recv_index = lax.all_to_all(send_index, ("row", "col"), split_axis=0, concat_axis=0, tiled=True)
    outgoing = solve(holders, depth, owned, interior_factor[0], coupling_panel[0], border_rows[0], target_rows)
    received = lax.all_to_all(
        outgoing.reshape(holders, depth, width), ("row", "col"), split_axis=0, concat_axis=0, tiled=True
    )
    return gather(recv_index.reshape(1, -1), received.reshape(holders * depth, width), border_block)


def solution(mesh):
    placed = (
        P("row", None, None),
        P("row", None, None),
        P("row", "col", None),
        P("row", "col"),
        P(("row", "col"), None),
    )
    return jax.shard_map(
        local, mesh=mesh, in_specs=placed, out_specs=P(("row", "col"), None), check_vma=False
    )
```

time: 299 us -> 75.4 us (0.25); the launches traced: 294 us -> 75.2 us
  other arithmetic: 140 us -> 2.4 us
  local copies, waits for them, and re-layouts: 51.3 us -> 7.63 us
  matrix products: 39 us -> 0 us
  Pallas kernels: 0 us -> 25.8 us
  waiting for transfers between devices: 48.6 us -> 26.2 us
    another operation x6 -> x0, other arithmetic: 127 us -> none  [the longest x4 127 us: substitute(): lax.linalg.triangular_solve(factor, forward, left_side=True, lower=True,...]
    another operation x45 -> x0, local copies, waits for them, and re-layouts: 41.5 us -> none
    another operation x46 -> x0, matrix products: 37 us -> none  [the longest x23 19.5 us: substitute(): lax.linalg.triangular_solve(factor, panel_cols, left_side=True, lower=True)]
    pallas_call x0 -> x2, Pallas kernels: none -> 25.8 us  [the longest x1 24.5 us: solve(): pl.pallas_call(functools.partial(solve_kernel, holders, depth, owned), ou...]
    all_to_all x2, waiting for transfers between devices: 48.6 us -> 26.2 us  [the longest x1 26.2 us: local(): lax.all_to_all(outgoing.reshape(holders, depth, width), ('row', 'col'), s...]
    scatter-add x1 -> x0, other arithmetic: 7.46 us -> none  [local(): jnp.zeros((owned_rows, panel_width), jnp.float32).at[recv_index.reshape(-1)]]
    gather x0 -> x2, local copies, waits for them, and re-layouts: none -> 6.95 us  [local(): wanted = targets[jnp.minimum(first, sent - 1)]]
    scatter x2 -> x0, local copies, waits for them, and re-layouts: 6.09 us -> none  [the longest x1 3.64 us: local(): jnp.zeros((holders * slot_depth, panel_width), jnp.float32).at[position]]
  transfers between devices with their start and end apart: 2 -> 2, of which waited for: 1 -> 1; matrix products, arithmetic and copies ran while one was open for 74% -> 2% of each run, Pallas kernels for 0% -> 33%
where the time goes in v1:
time: 75.4 us; the launch traced here: 75.2 us
  waiting for transfers between devices  26.2 us (35%)
  Pallas kernels  25.8 us (34%)
  starting transfers between devices  13.2 us (18%)
  local copies, waits for them, and re-layouts  7.63 us (10%)
  other arithmetic  2.4 us (3%)
    all_to_all x1, waiting for transfers between devices, local(): lax.all_to_all(outgoing.reshape(holders, depth, width), ('row', 'col'), s...  26.2 us
    pallas_call x1, Pallas kernels, solve(): pl.pallas_call(functools.partial(solve_kernel, holders, depth, owned), ou...  24.5 us
    all_to_all x1, starting transfers between devices, local(): lax.all_to_all(send_index, ('row', 'col'), split_axis=0, concat_axis=0, t...  7.33 us
    gather x2, local copies, waits for them, and re-layouts, local(): wanted = targets[jnp.minimum(first, sent - 1)]  6.95 us
    all_to_all x1, starting transfers between devices, local(): lax.all_to_all(outgoing.reshape(holders, depth, width), ('row', 'col'), s...  5.83 us
  transfers between devices with their start and end apart: 2, of which 1 were waited for; matrix products, arithmetic and copies ran while one was open for 2% of the time, Pallas kernels for 33%

profile of v1, /device:TPU:0, one launch (start us, length us, event | category | flops | bytes accessed | tf_op | source)
XLA Modules:
  0.0 75.2 jit_solution(14368889811856083724)
XLA Ops:
  0.0 0.0 copy-start.1
  0.0 0.8 %and_select_fusion.3 = s32[1,512]{1,0:T(1,128)S(1)} fusion(s32[1,512]{1,0:T(1,128)} %targets_ref.1), kind=kLoop, calls=%fused_computation.10 | loop fusion | flops 7680 | bytes 4096 | tf_op jit(solution)/shard_map/jit(floor_divide)/jit(_where)/select_n | solution.py:193
  0.8 0.1 convert_reduce_fusion
  0.9 0.1 compare_select_fusion
  1.0 0.1 reshape.171
  1.0 0.0 copy-done.1
  1.1 6.9 %gather_fusion = s32[1024]{0:T(1024)S(1)} fusion(s32[512]{0:T(512)S(1)} %bitcast.10, s32[1024]{0:T(1024)S(1)} %broadcast_clamp_fusion), kind=kCustom, calls=%fused_computation | custom fusion | bytes 12288 | tf_op jit(solution)/shard_map/gather | solution.py:197
  7.9 0.1 gather.7
  8.0 0.7 and_select_fusion.1
  8.8 7.3 %all-to-all-start = ((s32[32,1,32]{2,1,0:T(1,128)}), s32[32,1,32]{2,1,0:T(1,128)S(1)}, u32[]{:S(2)}, u32[]{:S(2)}) async-start(s32[32,1,32]{2,1,0:T(1,128)} %and_select_fusion.1), calls=%async_computation | async-start | bytes 32768 | tf_op jit(solution)/shard_map/all_to_all | solution.py:200
  16.1 24.5 %solve.1 = bf16[1024,512]{1,0:T(8,128)(2,1)} custom-call(f32[1536,1536]{1,0:T(8,128)} %bitcast.13, bf16[1536,512]{1,0:T(8,128)(2,1)} %bitcast.14, bf16[512,1536]{1,0:T(8,128)(2,1)} %bitcast.15, s32[1,512]{1,0:T(1,128)} %targets_ref.1), custom_call_target="tpu_custom_call" | custom-call | flops 10000000000 | bytes 14000000 | tf_op jit(solution)/shard_map/solve/pallas_call | solution.py:146
  40.6 0.0 copy-start
  40.6 0.0 all-to-all-done
  40.6 5.8 %all-to-all-start.1 = ((bf16[32,32,512]{2,1,0:T(8,128)(2,1)}), bf16[32,32,512]{2,1,0:T(8,128)(2,1)S(1)}, u32[]{:S(2)}, u32[]{:S(2)}) async-start(bf16[32,32,512]{2,1,0:T(8,128)(2,1)} %bitcast.11), calls=%async_computation.1 | async-start | bytes 2097152 | tf_op jit(solution)/shard_map/all_to_all | solution.py:202
  46.5 0.5 broadcast.189
  47.0 0.7 reduce.3
  47.7 0.1 reshape.166.index_ref
  47.7 26.2 %all-to-all-done.1 = bf16[32,32,512]{2,1,0:T(8,128)(2,1)S(1)} async-done(((bf16[32,32,512]{2,1,0:T(8,128)(2,1)}), bf16[32,32,512]{2,1,0:T(8,128)(2,1)S(1)}, u32[]{:S(2)}, u32[]{:S(2)}) %all-to-all-start.1) | async-done | bytes 1048608 | tf_op jit(solution)/shard_map/all_to_all | solution.py:202
  73.9 0.0 copy-done
  73.9 1.2 %gather.10 = f32[256,512]{1,0:T(8,128)} custom-call(s32[1,1024]{1,0:T(1,128)S(1)} %reshape.166.index_ref, bf16[1024,512]{1,0:T(8,128)(2,1)S(1)} %bitcast.9, f32[256,512]{1,0:T(8,128)S(1)} %copy-done), custom_call_target="tpu_custom_call" | custom-call | tf_op jit(solution)/shard_map/gather/pallas_call | solution.py:176
  (1 shorter events, 0.0 us)
Async XLA Ops:
  0.0 1.1 %copy-start.1 = (s32[1,512]{1,0:T(1,128)S(1)}, s32[1,512]{1,0:T(1,128)}, u32[]{:S(2)}) copy-start(s32[1,512]{1,0:T(1,128)} %targets_ref.1) | copy-start | bytes 6148
  8.8 31.9 %all-to-all-start = ((s32[32,1,32]{2,1,0:T(1,128)}), s32[32,1,32]{2,1,0:T(1,128)S(1)}, u32[]{:S(2)}, u32[]{:S(2)}) async-start(s32[32,1,32]{2,1,0:T(1,128)} %and_select_fusion.1), calls=%async_computation | async-start | bytes 32768 | tf_op jit(solution)/shard_map/all_to_all | solution.py:200
  40.6 33.3 %copy-start = (f32[256,512]{1,0:T(8,128)S(1)}, f32[256,512]{1,0:T(8,128)}, u32[]{:S(2)}) copy-start(f32[256,512]{1,0:T(8,128)} %block_ref.1) | copy-start | bytes 1572868
  40.6 33.3 %all-to-all-start.1 = ((bf16[32,32,512]{2,1,0:T(8,128)(2,1)}), bf16[32,32,512]{2,1,0:T(8,128)(2,1)S(1)}, u32[]{:S(2)}, u32[]{:S(2)}) async-start(bf16[32,32,512]{2,1,0:T(8,128)(2,1)} %bitcast.11), calls=%async_computation.1 | async-start | bytes 2097152 | tf_op jit(solution)/shard_map/all_to_all | solution.py:202

commit v2 on v1

--- a/solution.py
+++ b/solution.py
@@ -12,6 +12,7 @@
 BASE = 16
 LANES = 128
 BLOCK = 256
+COLUMNS = 256
 NN = (((1,), (0,)), ((), ()))
 TN = (((0,), (0,)), ((), ()))
 
@@ -121,88 +122,194 @@
     rows = targets.shape[1]
     holder = targets // owned
     ids = iota((holders, rows), 0)
-    counts = jnp.sum((ids == holder).astype(F32), axis=1, keepdims=True)
+    here = ids == holder
+    counts = jnp.sum(here.astype(F32), axis=1, keepdims=True)
     start = jnp.sum(jnp.where(ids < holder, counts, 0.0), axis=0, keepdims=True).astype(jnp.int32)
-    position = holder * depth + iota((1, rows), 1) - start
-    return iota((holders * depth, rows), 0) == position
-
-
-def solve_kernel(holders, depth, owned, factor_ref, panel_ref, border_ref, targets_ref, out_ref,
-                 small_ref, inv_hi, inv_lo, l_hi, l_lo, x_hi, x_lo, slots_ref):
-    slots = slots_of(targets_ref[...], holders, depth, owned)
-    slots_ref[...] = jnp.where(slots, 1.0, 0.0).astype(BF16)
+    rank = iota((1, rows), 1) - start
+    return holder * depth + rank, here, rank
+
+
+def flatten(blocks):
+    holders, depth, width = blocks.shape
+    if depth % 16:
+        return blocks.astype(F32).reshape(holders * depth, width).astype(blocks.dtype)
+    return blocks.reshape(holders * depth, width)
+
+
+def panel_kernel(dims, factor_hbm, panel_hbm, border_hbm, targets_ref, block_hbm, out_ref,
+                 factor_ref, panel_ref, border_ref, block_ref, small_ref, inv_hi, inv_lo, l_hi, l_lo,
+                 x_hi, x_lo, slots_ref, index_out, index_in, send_buf, recv_buf,
+                 load_sem, index_send, index_recv, send_sem, recv_sem):
+    n_row, n_col, depth = dims
+    holders = n_row * n_col
+    owned = block_ref.shape[0]
+    blocks = inv_hi.shape[0]
+    chunks, width = send_buf.shape[0], send_buf.shape[3]
+    me = lax.axis_index("row") * n_col + lax.axis_index("col")
+
+    def peer(step):
+        other = lax.rem(me + step, holders)
+        return other, (other // n_col, lax.rem(other, n_col))
+
+    barrier = pltpu.get_barrier_semaphore()
+
+    def greet(step, carry):
+        pl.semaphore_signal(barrier, inc=1, device_id=peer(step)[1], device_id_type=pl.DeviceIdType.MESH)
+        return carry
+
+    lax.fori_loop(1, holders, greet, 0)
+    diagonal, below = [], []
+    for k in range(blocks):
+        at = (pl.ds(k * BLOCK, BLOCK), pl.ds(k * BLOCK, BLOCK))
+        diagonal.append(pltpu.make_async_copy(factor_hbm.at[at], factor_ref.at[at], load_sem.at[k]))
+    for k in range(1, blocks):
+        at = (pl.ds(k * BLOCK, BLOCK), pl.ds(0, k * BLOCK))
+        below.append(pltpu.make_async_copy(factor_hbm.at[at], factor_ref.at[at], load_sem.at[blocks + k]))
+    panel_copy = pltpu.make_async_copy(panel_hbm, panel_ref, load_sem.at[blocks])
+    border_copy = pltpu.make_async_copy(border_hbm, border_ref, load_sem.at[2 * blocks])
+    block_copy = pltpu.make_async_copy(block_hbm, block_ref, load_sem.at[2 * blocks + 1])
+    for copy in diagonal + below + [panel_copy, border_copy, block_copy]:
+        copy.start()
+
+    position, here, rank = slots_of(targets_ref[...], holders, depth, owned)
+    rows = position.shape[1]
+    slots_ref[...] = jnp.where(iota((holders * depth, rows), 0) == position, 1.0, 0.0).astype(BF16)
+    within = (lax.rem(targets_ref[...], owned) + 1).astype(F32)
+    named = split(jnp.where(here, within, 0.0))
+    ranked = jnp.where(iota((LANES, rows), 0) % depth == rank, 1.0, 0.0).astype(BF16)
+    nt = (((1,), (1,)), ((), ()))
+    index = dot(named[0], ranked, nt) + dot(named[1], ranked, nt)
+    index_out[...] = jnp.broadcast_to(index[:, None, :], index_out.shape)
+
+    for copy in diagonal:
+        copy.wait()
     invert_bases(factor_ref, small_ref)
     invert_blocks(factor_ref, small_ref, inv_hi, inv_lo)
+    for copy in below:
+        copy.wait()
     split_factor(factor_ref, l_hi, l_lo)
-    substitute(lambda at: panel_ref[at, :], l_hi, l_lo, inv_hi, inv_lo, x_hi, x_lo)
-    update = dot(border_ref[...], x_hi[...]).astype(BF16)
-    out_ref[...] = dot(slots_ref[...], update).astype(BF16)
-
-
-def solve(holders, depth, owned, factor, panel, border, targets):
-    n, width = panel.shape
+
+    pl.semaphore_wait(barrier, holders - 1)
+
+    def index_copy(step):
+        other, place = peer(step)
+        return pltpu.make_async_remote_copy(
+            src_ref=index_out.at[other], dst_ref=index_in.at[me],
+            send_sem=index_send.at[other], recv_sem=index_recv.at[me],
+            device_id=place, device_id_type=pl.DeviceIdType.MESH,
+        )
+
+    def row_copy(chunk, step):
+        other, place = peer(step)
+        return pltpu.make_async_remote_copy(
+            src_ref=send_buf.at[chunk, other], dst_ref=recv_buf.at[chunk, me],
+            send_sem=send_sem.at[chunk, other], recv_sem=recv_sem.at[chunk, me],
+            device_id=place, device_id_type=pl.DeviceIdType.MESH,
+        )
+
+    def arrival(chunk, step):
+        other, place = peer(step)
+        return pltpu.make_async_remote_copy(
+            src_ref=send_buf.at[chunk, me], dst_ref=recv_buf.at[chunk, other],
+            send_sem=send_sem.at[chunk, me], recv_sem=recv_sem.at[chunk, other],
+            device_id=place, device_id_type=pl.DeviceIdType.MESH,
+        )
+
+    def index_arrival(step):
+        other, place = peer(step)
+        return pltpu.make_async_remote_copy(
+            src_ref=index_out.at[me], dst_ref=index_in.at[other],
+            send_sem=index_send.at[me], recv_sem=index_recv.at[other],
+            device_id=place, device_id_type=pl.DeviceIdType.MESH,
+        )
+
+    def each(act):
+        def body(step, carry):
+            act(step)
+            return carry
+
+        lax.fori_loop(1, holders, body, 0)
+
+    each(lambda step: index_copy(step).start())
+    index_in[me] = index_out[me]
+    panel_copy.wait()
+    border_copy.wait()
+
+    def one_chunk(chunk, carry):
+        columns = pl.ds(pl.multiple_of(chunk * width, LANES), width)
+        substitute(lambda at: panel_ref[at, columns], l_hi, l_lo, inv_hi, inv_lo, x_hi, x_lo)
+        update = dot(border_ref[...], x_hi[...]).astype(BF16)
+        packed = dot(slots_ref[...], update).reshape(holders, depth, width)
+        send_buf[chunk] = packed.astype(BF16)
+        each(lambda step: row_copy(chunk, step).start())
+        recv_buf[chunk, me] = send_buf[chunk, me]
+        return carry
+
+    lax.fori_loop(0, chunks, one_chunk, 0)
+
+    each(lambda step: index_arrival(step).wait_recv())
+    wide = jnp.concatenate([index_in[:, 0, :]] * (holders * depth // LANES), axis=1)
+    own = iota(wide.shape, 0) == iota(wide.shape, 1) // depth
+    wanted = jnp.sum(jnp.where(own, wide, 0.0), axis=0, keepdims=True)
+    pick = (iota((owned, holders * depth), 0) + 1).astype(F32) == wanted
+    pick = jnp.where(pick, 1.0, 0.0).astype(BF16)
+    block_copy.wait()
+    for chunk in range(chunks):
+        columns = pl.ds(chunk * width, width)
+        each(lambda step: arrival(chunk, step).wait_recv())
+        out_ref[:, columns] = block_ref[:, columns] - dot(pick, flatten(recv_buf[chunk]))
+    each(lambda step: index_copy(step).wait_send())
+    for chunk in range(chunks):
+        each(lambda step: row_copy(chunk, step).wait_send())
+
+
+def local(coupling_panel, interior_factor, border_rows, target_rows, border_block):
+    n_row, n_col = lax.axis_size("row"), lax.axis_size("col")
+    holders = n_row * n_col
+    factor, panel, border = interior_factor[0], coupling_panel[0], border_rows[0]
+    n, total = panel.shape
+    sent = border.shape[0]
+    depth = 2 * sent // holders
+    width = min(COLUMNS, total)
+    chunks = total // width
+    blocks = n // BLOCK
+    padded = -(-(n // LANES) // 8) * 8
+    hbm = pl.BlockSpec(memory_space=pl.ANY)
     vmem = pl.BlockSpec(memory_space=pltpu.VMEM)
-    padded = -(-(n // LANES) // 8) * 8
+    dma = pltpu.SemaphoreType.DMA
     return pl.pallas_call(
-        functools.partial(solve_kernel, holders, depth, owned),
-        out_shape=jax.ShapeDtypeStruct((holders * depth, width), BF16),
-        in_specs=[vmem] * 4,
+        functools.partial(panel_kernel, (n_row, n_col, depth)),
+        out_shape=jax.ShapeDtypeStruct(border_block.shape, F32),
+        in_specs=[hbm, hbm, hbm, vmem, hbm],
         out_specs=vmem,
         scratch_shapes=[
+            pltpu.VMEM((n, n), F32),
+            pltpu.VMEM((n, total), BF16),
+            pltpu.VMEM(border.shape, BF16),
+            pltpu.VMEM(border_block.shape, F32),
             pltpu.VMEM((BASE, padded, LANES), F32),
-            pltpu.VMEM((n // BLOCK, BLOCK, BLOCK), BF16),
-            pltpu.VMEM((n // BLOCK, BLOCK, BLOCK), BF16),
+            pltpu.VMEM((blocks, BLOCK, BLOCK), BF16),
+            pltpu.VMEM((blocks, BLOCK, BLOCK), BF16),
             pltpu.VMEM((n, n), BF16),
             pltpu.VMEM((n, n), BF16),
             pltpu.VMEM((n, width), BF16),
             pltpu.VMEM((n, width), BF16),
-            pltpu.VMEM((holders * depth, border.shape[0]), BF16),
+            pltpu.VMEM((holders * depth, sent), BF16),
+            pltpu.VMEM((holders, 8, LANES), F32),
+            pltpu.VMEM((holders, 8, LANES), F32),
+            pltpu.VMEM((chunks, holders, depth, width), BF16),
+            pltpu.VMEM((chunks, holders, depth, width), BF16),
+            dma((2 * blocks + 2,)),
+            dma((holders,)),
+            dma((holders,)),
+            dma((chunks, holders)),
+            dma((chunks, holders)),
         ],
-        compiler_params=pltpu.CompilerParams(vmem_limit_bytes=60 * 2**20),
-        cost_estimate=pl.CostEstimate(flops=10**10, bytes_accessed=14 * 10**6, transcendentals=0),
-        name="solve",
-    )(factor, panel, border, targets)
-
-
-def gather_kernel(owned, index_ref, received_ref, block_ref, out_ref):
-    slots = received_ref.shape[0]
-    pick = iota((owned, slots), 0) == index_ref[...]
-    pick = jnp.where(pick, 1.0, 0.0).astype(BF16)
-    out_ref[...] = block_ref[...] - dot(pick, received_ref[...])
-
-
-def gather(index, received, block):
-    vmem = pl.BlockSpec(memory_space=pltpu.VMEM)
-    return pl.pallas_call(
-        functools.partial(gather_kernel, block.shape[0]),
-        out_shape=jax.ShapeDtypeStruct(block.shape, F32),
-        in_specs=[vmem] * 3,
-        out_specs=vmem,
-        compiler_params=pltpu.CompilerParams(vmem_limit_bytes=40 * 2**20),
-        name="gather",
-    )(index, received, block)
-
-
-def local(coupling_panel, interior_factor, border_rows, target_rows, border_block):
-    holders = lax.axis_size("row") * lax.axis_size("col")
-    owned = border_block.shape[0]
-    targets = target_rows[0]
-    sent = targets.shape[0]
-    depth = 2 * sent // holders
-    width = border_block.shape[1]
-    holder_of = targets // owned
-    ids = jnp.arange(holders, dtype=jnp.int32)
-    start = jnp.sum((holder_of[None, :] < ids[:, None]).astype(jnp.int32), axis=1)
-    first = start[:, None] + jnp.arange(depth, dtype=jnp.int32)[None, :]
-    wanted = targets[jnp.minimum(first, sent - 1)]
-    valid = (first < sent) & (wanted // owned == ids[:, None])
-    send_index = jnp.where(valid, wanted % owned, -1)
-    recv_index = lax.all_to_all(send_index, ("row", "col"), split_axis=0, concat_axis=0, tiled=True)
-    outgoing = solve(holders, depth, owned, interior_factor[0], coupling_panel[0], border_rows[0], target_rows)
-    received = lax.all_to_all(
-        outgoing.reshape(holders, depth, width), ("row", "col"), split_axis=0, concat_axis=0, tiled=True
-    )
-    return gather(recv_index.reshape(1, -1), received.reshape(holders * depth, width), border_block)
+        compiler_params=pltpu.CompilerParams(
+            vmem_limit_bytes=60 * 2**20, collective_id=0, has_side_effects=True
+        ),
+        name="schur_panel",
+    )(factor, panel, border, target_rows, border_block)
 
 
 def solution(mesh):

time: 75.4 us -> 57.7 us (0.77)
  Pallas kernels: 25.8 us -> 55.6 us
  waiting for transfers between devices: 26.2 us -> 0 us
  starting transfers between devices: 13.2 us -> 0 us
  local copies, waits for them, and re-layouts: 7.63 us -> 1.87 us
  other arithmetic: 2.4 us -> 0 us
    pallas_call x2 -> x1, Pallas kernels: 25.8 us -> 55.6 us  [local(): pl.pallas_call(functools.partial(panel_kernel, (n_row, n_col, depth)), ou...]
    all_to_all x2 -> x0, waiting for transfers between devices: 26.2 us -> none  [the longest x1 26.2 us: local(): lax.all_to_all(outgoing.reshape(holders, depth, width), ('row', 'col'), s...]
    all_to_all x2 -> x0, starting transfers between devices: 13.2 us -> none  [the longest x1 7.33 us: local(): lax.all_to_all(send_index, ('row', 'col'), split_axis=0, concat_axis=0, t...]
    gather x2 -> x0, local copies, waits for them, and re-layouts: 6.95 us -> none  [local(): wanted = targets[jnp.minimum(first, sent - 1)]]
    unnamed x4 -> x1, local copies, waits for them, and re-layouts: 0.01 us -> 1.87 us
    select_n x3 -> x0, other arithmetic: 1.59 us -> none  [the longest x1 0.77 us: local(): holder_of = targets // owned]
  transfers between devices with their start and end apart: 2 -> 0, of which waited for: 1 -> 0; matrix products, arithmetic and copies ran while one was open for 2% -> 0% of each run, Pallas kernels for 33% -> 0%
where the time goes in v2:
time: 57.7 us; the launch traced here: 57.5 us
  Pallas kernels  55.6 us (96%)
  local copies, waits for them, and re-layouts  1.87 us (3%)
    pallas_call x1, Pallas kernels, local(): pl.pallas_call(functools.partial(panel_kernel, (n_row, n_col, depth)), ou...  55.6 us
    unnamed x1, local copies, waits for them, and re-layouts  1.87 us

profile of v2, /device:TPU:0, one launch (start us, length us, event | category | flops | bytes accessed | tf_op | source)
XLA Modules:
  0.0 57.5 jit_solution(18198604965251070423)
XLA Ops:
  0.0 55.6 %schur_panel.1 = f32[256,512]{1,0:T(8,128)} custom-call(f32[1536,1536]{1,0:T(8,128)} %bitcast.3, bf16[1536,512]{1,0:T(8,128)(2,1)} %bitcast.4, bf16[512,1536]{1,0:T(8,128)(2,1)} %bitcast.5, s32[1,512]{1,0:T(1,128)} %targets_ref.1, f32[256,512]{1,0:T(8,128)} %block_hbm.1), custom_call_target="tpu_custom_call" | custom-call | tf_op jit(solution)/shard_map/schur_panel/pallas_call | solution.py:280
  55.6 1.9 %copy.7 = f32[256,512]{1,0:T(8,128)} copy(f32[256,512]{1,0:T(8,128)} %schur_panel.1) | data formatting | bytes 1048576

commit v3 on v2

--- a/solution.py
+++ b/solution.py
@@ -69,29 +69,31 @@
 
 
 def invert_blocks(factor_ref, small_ref, inv_hi, inv_lo):
-    blocks = factor_ref.shape[0] // BLOCK
-    row, col = iota((BLOCK, BLOCK), 0), iota((BLOCK, BLOCK), 1)
-    per = BLOCK // LANES
+    chunks = factor_ref.shape[0] // LANES
+    row, col = iota((LANES, LANES), 0), iota((LANES, LANES), 1)
     inverses = []
-    for p in range(blocks):
-        parts = []
-        for h in range(per):
-            compact = small_ref[:, p * per + h, :]
-            parts.append(jnp.concatenate([compact] * (LANES // BASE), axis=0))
-        tall = jnp.concatenate(parts, axis=0)
-        wide = jnp.concatenate([tall] * per, axis=1)
-        inverses.append(jnp.where(row // BASE == col // BASE, wide, 0.0))
+    for k in range(chunks):
+        tall = jnp.concatenate([small_ref[:, k, :]] * (LANES // BASE), axis=0)
+        inverses.append(jnp.where(row // BASE == col // BASE, tall, 0.0))
     size = BASE
-    while size < BLOCK:
+    while size < LANES:
         off = (row // (2 * size) == col // (2 * size)) & (row // size != col // size) & (row > col)
-        for p in range(blocks):
-            here = pl.ds(p * BLOCK, BLOCK)
+        for k in range(chunks):
+            here = pl.ds(k * LANES, LANES)
             below = split(jnp.where(off, factor_ref[here, here], 0.0))
-            inverse = split(inverses[p])
-            inverses[p] = inverses[p] - dot3(inverse, split(dot3(below, inverse)))
+            inverse = split(inverses[k])
+            inverses[k] = inverses[k] - dot3(inverse, split(dot3(below, inverse)))
         size *= 2
-    for p in range(blocks):
-        inv_hi[p], inv_lo[p] = split(inverses[p])
+    none = jnp.zeros((LANES, LANES), BF16)
+    for p in range(chunks // 2):
+        first, second = split(inverses[2 * p]), split(inverses[2 * p + 1])
+        below = factor_ref[pl.ds((2 * p + 1) * LANES, LANES), pl.ds(2 * p * LANES, LANES)]
+        corner = split(-dot3(second, split(dot3(split(below), first))))
+        for part, ref in enumerate((inv_hi, inv_lo)):
+            ref[p, :LANES, :LANES] = first[part]
+            ref[p, :LANES, LANES:] = none
+            ref[p, LANES:, :LANES] = corner[part]
+            ref[p, LANES:, LANES:] = second[part]
 
 
 def split_factor(factor_ref, l_hi, l_lo):
@@ -254,13 +256,12 @@
     pick = (iota((owned, holders * depth), 0) + 1).astype(F32) == wanted
     pick = jnp.where(pick, 1.0, 0.0).astype(BF16)
     block_copy.wait()
+    each(lambda step: index_copy(step).wait_send())
     for chunk in range(chunks):
         columns = pl.ds(chunk * width, width)
+        each(lambda step: row_copy(chunk, step).wait_send())
         each(lambda step: arrival(chunk, step).wait_recv())
         out_ref[:, columns] = block_ref[:, columns] - dot(pick, flatten(recv_buf[chunk]))
-    each(lambda step: index_copy(step).wait_send())
-    for chunk in range(chunks):
-        each(lambda step: row_copy(chunk, step).wait_send())
 
 
 def local(coupling_panel, interior_factor, border_rows, target_rows, border_block):

time: 57.7 us -> 53.6 us (0.929)
  Pallas kernels: 55.6 us -> 51.5 us
    pallas_call x1, Pallas kernels: 55.6 us -> 51.5 us  [local(): pl.pallas_call(functools.partial(panel_kernel, (n_row, n_col, depth)), ou...]
where the time goes in v3:
time: 53.6 us; the launch traced here: 53.4 us
  Pallas kernels  51.5 us (96%)
  local copies, waits for them, and re-layouts  1.87 us (3%)
    pallas_call x1, Pallas kernels, local(): pl.pallas_call(functools.partial(panel_kernel, (n_row, n_col, depth)), ou...  51.5 us
    unnamed x1, local copies, waits for them, and re-layouts  1.87 us

profile of v3, /device:TPU:0, one launch (start us, length us, event | category | flops | bytes accessed | tf_op | source)
XLA Modules:
  0.0 53.4 jit_solution(11092160969229878055)
XLA Ops:
  0.0 51.5 %schur_panel.1 = f32[256,512]{1,0:T(8,128)} custom-call(f32[1536,1536]{1,0:T(8,128)} %bitcast.3, bf16[1536,512]{1,0:T(8,128)(2,1)} %bitcast.4, bf16[512,1536]{1,0:T(8,128)(2,1)} %bitcast.5, s32[1,512]{1,0:T(1,128)} %targets_ref.1, f32[256,512]{1,0:T(8,128)} %block_hbm.1), custom_call_target="tpu_custom_call" | custom-call | tf_op jit(solution)/shard_map/schur_panel/pallas_call | solution.py:281
  51.5 1.9 %copy.7 = f32[256,512]{1,0:T(8,128)} copy(f32[256,512]{1,0:T(8,128)} %schur_panel.1) | data formatting | bytes 1048576
